TPU v7x, 32 devices: a whole 2x2x4 slice. The times are simulated.
32 devices in a mesh: groups: 2 (over y), batch: 8 (over z, x), heads: 2 (over core).
Axes of the slice: x: 2, y: 2, z: 4, core: 2. Of those that a mesh axis runs over, the one named last changes fastest.
Arguments:
- storage: bfloat16 [1, 4096, 4608], P(None, ('groups', 'batch', 'heads')), parts along dimension 1, may hold values from -6 to 6
- block_table: int32 [4096], P('groups'), parts along dimension 0, may hold values from 0 to 2047, as said below
- lengths: int32 [16], P(('groups', 'batch')), parts along dimension 0, may hold values from 4 to 2048
- query: bfloat16 [16, 4, 128, 576], P(('groups', 'batch'), None, 'heads'), parts along dimension 0, may hold values from -10 to 10
Outputs:
- context: bfloat16 [16, 4, 128, 512], P(('groups', 'batch'), None, 'heads'), parts along dimension 0
There are 2 independent parts, one for each index of `groups`. A program takes and returns all parts, laid end to end along the dimension named above; each array names one. Nothing has to cross between parts.
Inputs may be any that keep to these rules, and one draw needn't show every extreme that they name: `block_table`: the entries are a permutation of 0 to 2047; entry g names block g mod 256 of sequence g // 256. Storage device k of the batch+heads order, with k = 2 b + p, holds for every batch index j exactly 16 blocks of sequences j * 1 to (j + 1) - 1, all with block numbers from p * 128 to (p + 1) * 128 - 1, in no particular order.
All inputs are finite; a program needn't handle non-finite values.
Results may differ from a plain program's by a relative error of at most 0.0031.
Values may be sent and summed in bfloat16 or wider, within the bound.
A program may use at most 64 MiB of HBM per device.

v0:
```python
import math

import jax
import jax.numpy as jnp
from jax import lax
from jax.sharding import PartitionSpec as P

LATENT = 512
ROPE = 64
HEAD_NOPE = 128
SEQ_DEV = 1
MAXLEN = 2048
BLK = 8
QTOK = 4


def partial_softmax(query_rows, key_rows, first_place, limits, score_scale):
    scores = (
        jnp.einsum("src,stc->srt", query_rows, key_rows, preferred_element_type=jnp.float32)
        * score_scale
    )
    places = first_place + jnp.arange(key_rows.shape[1], dtype=jnp.int32)
    visible = places[None, None, :] <= limits[:, :, None]
    masked = jnp.where(visible, scores, -1e30)
    highest = jnp.max(masked, axis=2)
    raised = jnp.where(visible, jnp.exp(masked - highest[:, :, None]), 0.0)
    totals = jnp.sum(raised, axis=2)
    mixed = jnp.einsum(
        "srt,stc->src",
        raised.astype(jnp.bfloat16),
        key_rows[:, :, :LATENT],
        preferred_element_type=jnp.float32,
    )
    return (highest, totals, mixed)


def local(storage, block_table, lengths, query):
    batch_count = lax.axis_size("batch")
    head_groups = lax.axis_size("heads")
    my_batch = lax.axis_index("batch")
    my_half = lax.axis_index("heads")
    slot_count = storage.shape[1]
    per_peer = slot_count // batch_count
    block_count = MAXLEN // BLK
    half_blocks = block_count // head_groups
    width = LATENT + ROPE
    zero_index = jnp.zeros((), jnp.int32)
    table_grid = block_table.reshape(batch_count, head_groups, slot_count)
    own_table = lax.dynamic_slice(
        table_grid, (my_batch, my_half, zero_index), (1, 1, slot_count)
    ).reshape(slot_count)
    owner = own_table // block_count // SEQ_DEV
    owner_table = (owner[:, None] == jnp.arange(batch_count, dtype=jnp.int32)[None, :]).astype(
        jnp.int32
    )
    rank = jnp.sum(owner_table * (jnp.cumsum(owner_table, axis=0) - 1), axis=1)
    send_place = owner * per_peer + rank
    order = (
        jnp.zeros((slot_count,), jnp.int32)
        .at[send_place]
        .set(jnp.arange(slot_count, dtype=jnp.int32))
    )
    outgoing = jnp.take(storage, order, axis=1)
    received = lax.all_to_all(outgoing, "batch", split_axis=1, concat_axis=1, tiled=True)
    sender_table = lax.dynamic_slice(
        table_grid, (zero_index, my_half, zero_index), (batch_count, 1, slot_count)
    ).reshape(batch_count, slot_count)
    sequence_ids = sender_table // block_count
    arrivals = sequence_ids // SEQ_DEV == my_batch
    arrive_place = (
        jnp.arange(batch_count, dtype=jnp.int32)[:, None] * per_peer
        + jnp.cumsum(arrivals.astype(jnp.int32), axis=1)
        - 1
    )
    target = (
        (sequence_ids - my_batch * SEQ_DEV) * half_blocks
        + sender_table % block_count
        - my_half * half_blocks
    )
    target = jnp.where(arrivals, target, slot_count)
    source = (
        jnp.zeros((slot_count,), jnp.int32)
        .at[target.reshape(-1)]
        .set(arrive_place.reshape(-1), mode="drop")
    )
    serving = jnp.take(received, source, axis=1)
    half_length = half_blocks * BLK
    seq_count = query.shape[0]
    local_keys = serving[0].reshape(seq_count, half_length * width)
    score_scale = 1.0 / math.sqrt(HEAD_NOPE + ROPE)
    every_query = lax.all_gather(query, "heads", axis=2, tiled=True)
    all_heads = every_query.shape[2]
    row_count = QTOK * all_heads
    query_rows = every_query.reshape(seq_count, row_count, width)
    draft = jnp.arange(row_count, dtype=jnp.int32) // all_heads
    limits = lengths[:, None] - QTOK + draft[None, :]
    key_rows = local_keys.reshape(seq_count, half_length, width)
    highest, totals, mixed = partial_softmax(
        query_rows, key_rows, my_half * half_length, limits, score_scale
    )
    shaped = (
        highest.reshape(1, seq_count, QTOK, all_heads),
        totals.reshape(1, seq_count, QTOK, all_heads),
        mixed.reshape(1, seq_count, QTOK, all_heads, LATENT),
    )
    pieces = (
        lax.all_to_all(shaped[0], "heads", split_axis=3, concat_axis=0, tiled=True),
        lax.all_to_all(shaped[1], "heads", split_axis=3, concat_axis=0, tiled=True),
        lax.all_to_all(shaped[2], "heads", split_axis=3, concat_axis=0, tiled=True),
    )
    overall = jnp.max(pieces[0], axis=0)
    factor = jnp.exp(pieces[0] - overall[None])
    totals = jnp.sum(pieces[1] * factor, axis=0)
    mixed = jnp.sum(pieces[2] * factor[..., None], axis=0)
    context = (mixed / totals[..., None]).astype(jnp.bfloat16)
    return context


def solution(mesh):
    in_specs = (
        P(None, ("groups", "batch", "heads"), None),
        P("groups"),
        P(("groups", "batch")),
        P(("groups", "batch"), None, "heads", None),
    )
    out_specs = P(("groups", "batch"), None, "heads", None)
    return jax.shard_map(local, mesh=mesh, in_specs=in_specs, out_specs=out_specs, check_vma=False)
```

profile of v0, /device:TPU:1, one launch (start us, length us, event | category | flops | bytes accessed | tf_op | source)
XLA Modules:
  0.0 96.4 jit_solution(5310189866146171281)
XLA Ops:
  3.0 1.0 %scatter_custom_fusion = s32[128]{0:T(128)S(1)} fusion(s32[128]{0:T(128)S(1)} %fusion.14, s32[128]{0:T(128)S(1)} %iota.24, s32[]{:T(128)} %constant.113.clone.1), kind=kCustom, calls=%fused_computation.74 | custom fusion | bytes 516 | tf_op jit(solution)/shard_map/scatter | solution.py:61
  4.1 4.3 %scatter_custom_fusion.1 = s32[128]{0:T(128)S(1)} fusion(s32[1024]{0:T(1024)S(1)} %bitcast.119, s32[1024]{0:T(1024)S(1)} %add_bitcast_fusion, s32[]{:T(128)} %constant.113.clone.1), kind=kCustom, calls=%fused_computation.72 | custom fusion | bytes 516 | tf_op jit(solution)/shard_map/scatter | solution.py:84
  8.4 1.3 %gather_fusion = bf16[128,4608]{1,0:T(8,128)(2,1)S(1)} fusion(bf16[128,4608]{1,0:T(8,128)(2,1)S(1)} %bitcast.103, s32[1024]{0:T(1024)S(1)} %pad_clamp_fusion.1), kind=kCustom, calls=%fused_computation.clone | custom fusion | bytes 2359808 | tf_op jit(solution)/shard_map/jit(_take)/gather | solution.py:63
  9.9 1.8 %copy.20 = bf16[1,128,4608]{2,0,1:T(2,128)(2,1)S(1)} copy(bf16[1,128,4608]{2,1,0:T(8,128)(2,1)S(1)} %bitcast_select_fusion.1) | data formatting | bytes 2359296 | tf_op jit(solution)/shard_map/jit(_take)/select_n | solution.py:63
  12.2 8.8 %reduce.8 = bf16[128,4608]{1,0:T(8,128)(2,1)} reduce(bf16[128,1,4608]{2,1,0:T(2,128)(2,1)S(1)} %bitcast.105, bf16[]{:T(256)} %broadcast.454), dimensions={1}, to_apply=%bitcast.102.reduce_sub_computation | reduce | bytes 2359298
  21.0 2.7 %reshape.485 = bf16[8,2,36864]{2,1,0:T(2,128)(2,1)} reshape(bf16[128,4608]{1,0:T(8,128)(2,1)} %reduce.8) | data formatting | bytes 2359296
  23.8 6.5 %all-to-all-start = ((bf16[8,2,36864]{2,1,0:T(2,128)(2,1)}), bf16[8,2,36864]{2,1,0:T(2,128)(2,1)S(1)}, u32[]{:S(2)}, u32[]{:S(2)}) async-start(bf16[8,2,36864]{2,1,0:T(2,128)(2,1)} %reshape.485), calls=%async_computation | async-start | bytes 2359296 | tf_op jit(solution)/shard_map/all_to_all | solution.py:64
  31.0 3.2 %all_gather.3 = bf16[1,4,128,576]{3,2,1,0:T(8,128)(2,1)} all-gather(bf16[1,4,64,576]{3,2,1,0:T(8,128)(2,1)S(1)} %copy-done.3), channel_id=1, replica_groups=mesh['groups'=2,'batch'=8,'heads'=2] {'heads'}, dimensions={2}, use_global_device_ids=true | all-gather | bytes 884736 | tf_op jit(solution)/shard_map/all_gather | solution.py:91
  34.2 23.9 %all-to-all-done = bf16[8,2,36864]{2,1,0:T(2,128)(2,1)S(1)} async-done(((bf16[8,2,36864]{2,1,0:T(2,128)(2,1)}), bf16[8,2,36864]{2,1,0:T(2,128)(2,1)S(1)}, u32[]{:S(2)}, u32[]{:S(2)}) %all-to-all-start) | async-done | bytes 1179680 | tf_op jit(solution)/shard_map/all_to_all | solution.py:64
  58.0 3.6 %reshape.486 = bf16[128,1,4608]{2,1,0:T(2,128)(2,1)} reshape(bf16[8,2,36864]{2,1,0:T(2,128)(2,1)S(1)} %all-to-all-done) | data formatting | bytes 2359296
  61.6 1.8 %copy.19 = bf16[1,128,4608]{2,1,0:T(8,128)(2,1)S(1)} copy(bf16[1,128,4608]{2,0,1:T(2,128)(2,1)} %bitcast.106) | data formatting | bytes 2359296
  63.4 1.3 %gather_fusion.1 = bf16[128,4608]{1,0:T(8,128)(2,1)S(1)} fusion(bf16[128,4608]{1,0:T(8,128)(2,1)S(1)} %bitcast.104, s32[1024]{0:T(1024)S(1)} %pad_clamp_fusion), kind=kCustom, calls=%fused_computation.1.clone | custom fusion | bytes 2359808 | tf_op jit(solution)/shard_map/jit(_take)/gather | solution.py:86
  64.9 1.9 %reshape.428 = bf16[1024,576]{1,0:T(8,128)(2,1)} reshape(bf16[1,128,4608]{2,1,0:T(8,128)(2,1)S(1)} %bitcast_select_fusion) | data formatting | bytes 2359296 | tf_op jit(solution)/shard_map/reshape.5
  66.8 1.9 %reshape_reshape_squeeze.3 = bf16[1,1024,576]{2,1,0:T(8,128)(2,1)} reshape(bf16[1,128,4608]{2,1,0:T(8,128)(2,1)S(1)} %bitcast_select_fusion) | data formatting | bytes 2359296 | tf_op jit(solution)/shard_map/reshape;reshape;squeeze | solution.py:97
  68.7 2.5 %fusion = (f32[512]{0:T(512)S(1)}, f32[1024,512]{0,1:T(8,128)S(1)}) fusion(s32[1024]{0:T(1024)S(1)} %iota_add_fusion, s32[512]{0:T(512)S(1)} %fusion.10, bf16[1024,576]{1,0:T(8,128)(2,1)} %reshape.428, bf16[512,576]{1,0:T(8,128)(2,1)S(1)} %bitcast.112), kind=kOutput, calls=%fused_computation.6 | convolution fusion | flops 606076416 | bytes 3874816 | tf_op jit(solution)/shard_map/src,stc->srt/dot_general | solution.py:19
  71.1 1.6 %fusion.1 = (f32[512]{0:T(512)S(1)}, bf16[512,1024]{1,0:T(8,128)(2,1)}) fusion(f32[1024,512]{0,1:T(8,128)S(1)} %get-tuple-element.11, f32[512]{0:T(512)S(1)} %get-tuple-element.10, s32[1024]{0:T(1024)S(1)} %iota_add_fusion, s32[512]{0:T(512)S(1)} %fusion.10), kind=kLoop, calls=%fused_computation.8 | loop fusion | flops 3669504 | bytes 3155968 | tf_op jit(solution)/shard_map/reduce_sum | solution.py:27
  73.4 0.8 reduce.11
  74.3 5.1 %all_to_all.62 = f32[2,1,256]{2,1,0:T(1,128)S(1)} all-to-all(f32[2,1,256]{2,1,0:T(1,128)S(1)} %reshape.489), channel_id=1, replica_groups=mesh['groups'=2,'batch'=8,'heads'=2] {'heads'}, dimensions={0} | all-to-all | bytes 4096 | tf_op jit(solution)/shard_map/all_to_all | solution.py:108
  80.4 0.8 reduce.9
  81.3 3.7 %all_to_all.63 = f32[2,1,256]{2,1,0:T(1,128)S(1)} all-to-all(f32[2,1,256]{2,1,0:T(1,128)S(1)} %reshape.487), channel_id=1, replica_groups=mesh['groups'=2,'batch'=8,'heads'=2] {'heads'}, dimensions={0} | all-to-all | bytes 4096 | tf_op jit(solution)/shard_map/all_to_all | solution.py:107
  85.8 1.9 %convolution_bitcast_fusion = f32[1,1,4,128,512]{4,3,2,1,0:T(8,128)S(1)} fusion(bf16[4,128,1024]{2,1,0:T(8,128)(2,1)} %bitcast.111, bf16[1,1024,576]{2,1,0:T(8,128)(2,1)S(1)} %copy-done.1), kind=kOutput, calls=%fused_computation.7 | convolution fusion | flops 536870912 | bytes 3145728 | tf_op jit(solution)/shard_map/srt,stc->src/dot_general | solution.py:28
  87.7 1.7 %copy.12 = f32[1,1,4,128,512]{4,2,1,0,3:T(4,128)} copy(f32[1,1,4,128,512]{4,3,2,1,0:T(8,128)S(1)} %convolution_bitcast_fusion) | data formatting | bytes 2097152 | tf_op jit(solution)/shard_map/srt,stc->src/dot_general | solution.py:28
  89.4 3.9 %all-to-all-start.1 = ((f32[1,1,4,128,512]{4,2,1,0,3:T(4,128)}), f32[1,1,4,128,512]{4,2,1,0,3:T(4,128)S(1)}, u32[]{:S(2)}, u32[]{:S(2)}) async-start(f32[1,1,4,128,512]{4,2,1,0,3:T(4,128)} %copy.12), calls=%async_computation.1 | async-start | bytes 2097152 | tf_op jit(solution)/shard_map/all_to_all | solution.py:109
  93.4 1.7 %all-to-all-done.1 = f32[1,1,4,128,512]{4,2,1,0,3:T(4,128)S(1)} async-done(((f32[1,1,4,128,512]{4,2,1,0,3:T(4,128)}), f32[1,1,4,128,512]{4,2,1,0,3:T(4,128)S(1)}, u32[]{:S(2)}, u32[]{:S(2)}) %all-to-all-start.1) | async-done | bytes 1048608 | tf_op jit(solution)/shard_map/all_to_all | solution.py:109
  (44 shorter events, 7.9 us)
Async XLA Ops:
  0.0 8.4 %copy-start = (bf16[1,128,4608]{2,1,0:T(8,128)(2,1)S(1)}, bf16[1,128,4608]{2,1,0:T(8,128)(2,1)}, u32[]{:S(2)}) copy-start(bf16[1,128,4608]{2,1,0:T(8,128)(2,1)} %param.6) | copy-start | bytes 3538948
  23.8 7.2 %copy-start.3 = (bf16[1,4,64,576]{3,2,1,0:T(8,128)(2,1)S(1)}, bf16[1,4,64,576]{3,2,1,0:T(8,128)(2,1)}, u32[]{:S(2)}) copy-start(bf16[1,4,64,576]{3,2,1,0:T(8,128)(2,1)} %param.9) | copy-start | bytes 884740
  23.8 34.2 %all-to-all-start = ((bf16[8,2,36864]{2,1,0:T(2,128)(2,1)}), bf16[8,2,36864]{2,1,0:T(2,128)(2,1)S(1)}, u32[]{:S(2)}, u32[]{:S(2)}) async-start(bf16[8,2,36864]{2,1,0:T(2,128)(2,1)} %reshape.485), calls=%async_computation | async-start | bytes 2359296 | tf_op jit(solution)/shard_map/all_to_all | solution.py:64
  66.8 1.9 %copy-start.2 = (bf16[1,4,128,576]{3,2,1,0:T(8,128)(2,1)S(1)}, bf16[1,4,128,576]{3,2,1,0:T(8,128)(2,1)}, u32[]{:S(2)}) copy-start(bf16[1,4,128,576]{3,2,1,0:T(8,128)(2,1)} %all_gather.3) | copy-start | bytes 1769476
  71.1 14.7 %copy-start.1 = (bf16[1,1024,576]{2,1,0:T(8,128)(2,1)S(1)}, bf16[1,1024,576]{2,1,0:T(8,128)(2,1)}, u32[]{:S(2)}) copy-start(bf16[1,1024,576]{2,1,0:T(8,128)(2,1)} %reshape_reshape_squeeze.3) | copy-start | bytes 3538948
  89.4 5.7 %all-to-all-start.1 = ((f32[1,1,4,128,512]{4,2,1,0,3:T(4,128)}), f32[1,1,4,128,512]{4,2,1,0,3:T(4,128)S(1)}, u32[]{:S(2)}, u32[]{:S(2)}) async-start(f32[1,1,4,128,512]{4,2,1,0,3:T(4,128)} %copy.12), calls=%async_computation.1 | async-start | bytes 2097152 | tf_op jit(solution)/shard_map/all_to_all | solution.py:109
where the time goes:
time: 97.3 us; the launch traced here: 96.4 us
  local copies, waits for them, and re-layouts  25.7 us (26%)
  waiting for transfers between devices  25.6 us (26%)
  other arithmetic  17.4 us (18%)
  blocking collectives  12 us (12%)
  starting transfers between devices  10.4 us (11%)
  matrix products  4.38 us (5%)
    all_to_all x1, waiting for transfers between devices, local(): lax.all_to_all(outgoing, 'batch', split_axis=1, concat_axis=1, tiled=True)  23.9 us
    unnamed x3, other arithmetic  10.5 us
    unnamed x17, local copies, waits for them, and re-layouts  9.66 us
    all_to_all x1, starting transfers between devices, local(): lax.all_to_all(outgoing, 'batch', split_axis=1, concat_axis=1, tiled=True)  6.47 us
    all_to_all x1, blocking collectives, local(): lax.all_to_all(shaped[1], 'heads', split_axis=3, concat_axis=0, tiled=True)  5.12 us
    scatter x1, local copies, waits for them, and re-layouts, local(): source = jnp.zeros((slot_count,), jnp.int32).at[target.reshape(-1)].set(a...  4.3 us
    all_to_all x1, starting transfers between devices, local(): lax.all_to_all(shaped[2], 'heads', split_axis=3, concat_axis=0, tiled=True)  3.92 us
    all_to_all x1, blocking collectives, local(): lax.all_to_all(shaped[0], 'heads', split_axis=3, concat_axis=0, tiled=True)  3.7 us
  transfers between devices with their start and end apart: 2, of which 2 were waited for; matrix products, arithmetic and copies ran while one was open for 0% of the time, Pallas kernels for 0%

commit v1 on v0

--- a/solution.py
+++ b/solution.py
@@ -1,10 +1,15 @@
+import functools
 import math
 
 import jax
 import jax.numpy as jnp
 from jax import lax
+from jax.experimental import pallas as pl
+from jax.experimental.pallas import tpu as pltpu
 from jax.sharding import PartitionSpec as P
 
+MESH = pl.DeviceIdType.MESH
+NT = (((1,), (1,)), ((), ()))
 LATENT = 512
 ROPE = 64
 HEAD_NOPE = 128
@@ -34,7 +39,7 @@
     return (highest, totals, mixed)
 
 
-def local(storage, block_table, lengths, query):
+def plain_local(storage, block_table, lengths, query):
     batch_count = lax.axis_size("batch")
     head_groups = lax.axis_size("heads")
     my_batch = lax.axis_index("batch")
@@ -116,6 +121,222 @@
     return context
 
 
+def fused_kernel(
+    batch_count, table_ref, length_ref, storage_ref, query_ref, out_ref,
+    stored, asked, outgoing, keys, query_even, query_odd,
+    load_sem, send_sem, recv_sem, pass_sem, take_sem,
+):
+    slot_count = stored.shape[0]
+    per_peer = slot_count // batch_count
+    block_count = MAXLEN // BLK
+    width = LATENT + ROPE
+    wide = query_even.shape[1]
+    me = lax.axis_index("batch")
+    half = lax.axis_index("heads")
+    sibling = 1 - half
+
+    def partner(step):
+        other = me
+        bit = 1
+        while bit < batch_count:
+            if step & bit:
+                other = other + bit * (1 - 2 * ((me // bit) % 2))
+            bit *= 2
+        return other
+
+    load_storage = pltpu.make_async_copy(storage_ref, stored, load_sem.at[0])
+    load_query = pltpu.make_async_copy(query_ref, asked, load_sem.at[1])
+    load_storage.start()
+    load_query.start()
+    barrier = pltpu.get_barrier_semaphore()
+    for step in range(1, batch_count):
+        pl.semaphore_signal(
+            barrier, inc=1, device_id={"batch": partner(step)}, device_id_type=MESH
+        )
+    pl.semaphore_signal(barrier, inc=1, device_id={"heads": sibling}, device_id_type=MESH)
+
+    table = table_ref[...]
+    device_count = table.shape[0]
+    row_ids = lax.broadcasted_iota(jnp.int32, table.shape, 0)
+    square = (slot_count, slot_count)
+    down = lax.broadcasted_iota(jnp.int32, square, 0)
+    across = lax.broadcasted_iota(jnp.int32, square, 1)
+    earlier = (down < across).astype(jnp.float32).astype(jnp.bfloat16)
+    own = jnp.sum(jnp.where(row_ids == 2 * me + half, table, 0), axis=0, keepdims=True)
+    owner = own // block_count
+    belongs = (row_ids == owner).astype(jnp.float32)
+    counts = jnp.dot(belongs.astype(jnp.bfloat16), earlier, preferred_element_type=jnp.float32)
+    rank = jnp.sum(belongs * counts, axis=0, keepdims=True).astype(jnp.int32)
+    place = owner * per_peer + rank
+    order = (down == place).astype(jnp.float32).astype(jnp.bfloat16)
+    load_storage.wait()
+    piece = 4 * 128
+    for first in range(0, stored.shape[1], piece):
+        outgoing[:, first : first + piece] = jnp.dot(
+            order, stored[:, first : first + piece], preferred_element_type=jnp.float32
+        ).astype(jnp.bfloat16)
+    pl.semaphore_wait(barrier, batch_count)
+
+    def rows(index):
+        return pl.ds(pl.multiple_of(index * per_peer, per_peer), per_peer)
+
+    def send(step):
+        other = partner(step)
+        return pltpu.make_async_remote_copy(
+            src_ref=outgoing.at[rows(other)],
+            dst_ref=keys.at[0, rows(me)],
+            send_sem=send_sem.at[step],
+            recv_sem=recv_sem.at[step],
+            device_id={"batch": other},
+            device_id_type=MESH,
+        )
+
+    def arrival(step):
+        other = partner(step)
+        return pltpu.make_async_remote_copy(
+            src_ref=outgoing.at[rows(other)],
+            dst_ref=keys.at[0, rows(other)],
+            send_sem=send_sem.at[step],
+            recv_sem=recv_sem.at[step],
+            device_id={"batch": other},
+            device_id_type=MESH,
+        )
+
+    def hand_over(step):
+        other = partner(step)
+        source = outgoing.at[rows(me)] if step == 0 else keys.at[0, rows(other)]
+        return pltpu.make_async_remote_copy(
+            src_ref=source,
+            dst_ref=keys.at[1, rows(other)],
+            send_sem=pass_sem.at[step],
+            recv_sem=take_sem.at[step],
+            device_id={"heads": sibling},
+            device_id_type=MESH,
+        )
+
+    steps = list(range(batch_count - 1, 0, -1))
+    for step in steps:
+        send(step).start()
+    hand_over(0).start()
+    keep = pltpu.make_async_copy(outgoing.at[rows(me)], keys.at[0, rows(me)], load_sem.at[2])
+    keep.start()
+
+    mine = table // block_count == me
+    marks = mine.astype(jnp.float32)
+    ranks = jnp.dot(
+        marks.astype(jnp.bfloat16), earlier, preferred_element_type=jnp.float32
+    ).astype(jnp.int32)
+    targets = jnp.where(mine, (row_ids // 2) * per_peer + ranks, -1)
+    blocks = (table % block_count).astype(jnp.float32).astype(jnp.bfloat16)
+    by_half = [jnp.zeros((1, slot_count), jnp.float32) for _ in range(2)]
+    for index in range(device_count):
+        pick = (down == targets[index : index + 1]).astype(jnp.float32).astype(jnp.bfloat16)
+        by_half[index % 2] += lax.dot_general(
+            blocks[index : index + 1], pick, NT, preferred_element_type=jnp.float32
+        )
+    first_half = half == 0
+    numbers = jnp.concatenate(
+        [
+            jnp.where(first_half, by_half[0], by_half[1]),
+            jnp.where(first_half, by_half[1], by_half[0]),
+        ],
+        axis=1,
+    ).astype(jnp.int32)
+    row_count = asked.shape[0]
+    heads = row_count // QTOK
+    draft = lax.broadcasted_iota(jnp.int32, (row_count, 1), 0) // heads
+    limits = length_ref[0] - QTOK + draft
+
+    load_query.wait()
+    space = wide - width
+    query_even[:, :width] = asked[...]
+    query_even[:, width:] = jnp.zeros((row_count, space), jnp.bfloat16)
+    query_odd[:, space:] = asked[...]
+    query_odd[:, :space] = jnp.zeros((row_count, space), jnp.bfloat16)
+
+    for step in steps:
+        arrival(step).wait_recv()
+        hand_over(step).start()
+    keep.wait()
+    for step in [0] + steps:
+        hand_over(step).wait_recv()
+
+    factor = math.log2(math.e) / math.sqrt(HEAD_NOPE + ROPE)
+    both = 2 * slot_count
+    scores = []
+    for i in range(BLK):
+        low = i * width // 128 * 128
+        queries = query_odd if i % 2 else query_even
+        part = keys[:, :, low : low + wide].reshape(both, wide)
+        dots = lax.dot_general(queries[...], part, NT, preferred_element_type=jnp.float32)
+        visible = numbers * BLK + i <= limits
+        scores.append(jnp.where(visible, dots, -1e30))
+    peak = functools.reduce(jnp.maximum, scores)
+    peak = jnp.max(peak, axis=1, keepdims=True)
+    totals = jnp.zeros((row_count, both), jnp.float32)
+    mixed_even = jnp.zeros((row_count, LATENT), jnp.float32)
+    mixed_odd = jnp.zeros((row_count, wide), jnp.float32)
+    for i in range(BLK):
+        low = i * width // 128 * 128
+        raised = jnp.exp2((scores[i] - peak) * factor)
+        totals += raised
+        weights = raised.astype(jnp.bfloat16)
+        if i % 2:
+            part = keys[:, :, low : low + wide].reshape(both, wide)
+            mixed_odd += jnp.dot(weights, part, preferred_element_type=jnp.float32)
+        else:
+            part = keys[:, :, low : low + LATENT].reshape(both, LATENT)
+            mixed_even += jnp.dot(weights, part, preferred_element_type=jnp.float32)
+    total = jnp.sum(totals, axis=1, keepdims=True)
+    mixed = mixed_even + mixed_odd[:, space : space + LATENT]
+    out_ref[...] = (mixed / total).astype(out_ref.dtype)
+    for step in steps:
+        send(step).wait_send()
+    for step in [0] + steps:
+        hand_over(step).wait_send()
+
+
+def local(storage, block_table, lengths, query):
+    batch_count = lax.axis_size("batch")
+    slot_count = storage.shape[1]
+    per_peer = slot_count // batch_count
+    whole = batch_count & (batch_count - 1) == 0 and query.shape[0] == SEQ_DEV
+    if per_peer % 16 or slot_count % 128 or not whole:
+        return plain_local(storage, block_table, lengths, query)
+    width = LATENT + ROPE
+    heads = query.shape[2]
+    row_count = QTOK * heads
+    wide = -(-width // 128) * 128
+    vmem = pl.BlockSpec(memory_space=pltpu.VMEM)
+    anywhere = pl.BlockSpec(memory_space=pl.ANY)
+    context = pl.pallas_call(
+        functools.partial(fused_kernel, batch_count),
+        out_shape=jax.ShapeDtypeStruct((row_count, LATENT), jnp.bfloat16),
+        in_specs=[vmem, pl.BlockSpec(memory_space=pltpu.SMEM), anywhere, anywhere],
+        out_specs=vmem,
+        scratch_shapes=[
+            pltpu.VMEM((slot_count, BLK * width), jnp.bfloat16),
+            pltpu.VMEM((row_count, width), jnp.bfloat16),
+            pltpu.VMEM((slot_count, BLK * width), jnp.bfloat16),
+            pltpu.VMEM((2, slot_count, BLK * width), jnp.bfloat16),
+            pltpu.VMEM((row_count, wide), jnp.bfloat16),
+            pltpu.VMEM((row_count, wide), jnp.bfloat16),
+            pltpu.SemaphoreType.DMA((3,)),
+            pltpu.SemaphoreType.DMA((batch_count,)),
+            pltpu.SemaphoreType.DMA((batch_count,)),
+            pltpu.SemaphoreType.DMA((batch_count,)),
+            pltpu.SemaphoreType.DMA((batch_count,)),
+        ],
+        compiler_params=pltpu.CompilerParams(collective_id=0, has_side_effects=True),
+    )(
+        block_table.reshape(-1, slot_count),
+        lengths,
+        storage[0],
+        query.reshape(row_count, width),
+    )
+    return context.reshape(1, QTOK, heads, LATENT)
+
+
 def solution(mesh):
     in_specs = (
         P(None, ("groups", "batch", "heads"), None),

time: 97.3 us -> 40.3 us (0.41)
  Pallas kernels: 0 us -> 37.8 us
  waiting for transfers between devices: 25.6 us -> 0 us
  local copies, waits for them, and re-layouts: 25.7 us -> 1.67 us
  other arithmetic: 17.4 us -> 0 us
  blocking collectives: 12 us -> 0 us
  starting transfers between devices: 10.4 us -> 0 us
  matrix products: 4.38 us -> 0 us
    pallas_call x0 -> x1, Pallas kernels: none -> 37.8 us  [local(): pl.pallas_call(functools.partial(fused_kernel, batch_count), out_shape=ja...]
    all_to_all x2 -> x0, waiting for transfers between devices: 25.6 us -> none  [the longest x1 23.9 us: local(): lax.all_to_all(outgoing, 'batch', split_axis=1, concat_axis=1, tiled=True)]
    unnamed x3 -> x0, other arithmetic: 10.5 us -> none
    all_to_all x2 -> x0, starting transfers between devices: 10.4 us -> none  [the longest x1 6.47 us: local(): lax.all_to_all(outgoing, 'batch', split_axis=1, concat_axis=1, tiled=True)]
    all_to_all x2 -> x0, blocking collectives: 8.82 us -> none  [the longest x1 5.12 us: local(): lax.all_to_all(shaped[1], 'heads', split_axis=3, concat_axis=0, tiled=True)]
    unnamed x17 -> x1, local copies, waits for them, and re-layouts: 9.66 us -> 1.67 us
    scatter x2 -> x0, local copies, waits for them, and re-layouts: 5.27 us -> none  [the longest x1 4.3 us: local(): source = jnp.zeros((slot_count,), jnp.int32).at[target.reshape(-1)].set(a...]
    dot_general x2 -> x0, matrix products: 4.38 us -> none  [the longest x1 2.45 us: partial_softmax(): jnp.einsum('src,stc->srt', query_rows, key_rows, preferred_element_type=j...]
  transfers between devices with their start and end apart: 2 -> 0, of which waited for: 2 -> 0; matrix products, arithmetic and copies ran while one was open for 0% -> 0% of each run, Pallas kernels for 0% -> 0%
where the time goes in v1:
time: 40.3 us; the launch traced here: 40.1 us
  Pallas kernels  37.8 us (94%)
  local copies, waits for them, and re-layouts  1.67 us (4%)
  between operations  0.66 us (2%)
    pallas_call x1, Pallas kernels, local(): pl.pallas_call(functools.partial(fused_kernel, batch_count), out_shape=ja...  37.8 us
    unnamed x1, local copies, waits for them, and re-layouts  1.67 us

profile of v1, /device:TPU:1, one launch (start us, length us, event | category | flops | bytes accessed | tf_op | source)
XLA Modules:
  0.0 40.1 jit_solution(3608220060365634397)
XLA Ops:
  0.7 37.8 %shard_map.46 = bf16[256,512]{1,0:T(8,128)(2,1)} custom-call(s32[16,128]{1,0:T(8,128)} %bitcast.7, s32[1]{0:T(128)S(6)} %copy.6.length_ref, bf16[128,4608]{1,0:T(8,128)(2,1)} %bitcast.4, bf16[256,576]{1,0:T(8,128)(2,1)} %bitcast.6), custom_call_target="tpu_custom_call" | custom-call | tf_op jit(solution)/shard_map/pallas_call | solution.py:312
  38.4 1.7 %copy.7 = bf16[1,4,64,512]{3,2,1,0:T(8,128)(2,1)} copy(bf16[1,4,64,512]{3,2,1,0:T(8,128)(2,1)} %bitcast.5) | data formatting | bytes 524288

commit v2 on v1

--- a/solution.py
+++ b/solution.py
@@ -123,8 +123,8 @@
 
 def fused_kernel(
     batch_count, table_ref, length_ref, storage_ref, query_ref, out_ref,
-    stored, asked, outgoing, keys, query_even, query_odd,
-    load_sem, send_sem, recv_sem, pass_sem, take_sem,
+    tabled, lengthy, stored, asked, outgoing, keys, query_even, query_odd,
+    load_sem, fetch_sem, send_sem, recv_sem, pass_sem, take_sem,
 ):
     slot_count = stored.shape[0]
     per_peer = slot_count // batch_count
@@ -144,10 +144,24 @@
             bit *= 2
         return other
 
-    load_storage = pltpu.make_async_copy(storage_ref, stored, load_sem.at[0])
+    pieces = BLK // 2
+    span = 2 * width
+
+    def columns(piece):
+        return pl.ds(piece * span, span)
+
+    load_table = pltpu.make_async_copy(table_ref, tabled, load_sem.at[0])
     load_query = pltpu.make_async_copy(query_ref, asked, load_sem.at[1])
-    load_storage.start()
-    load_query.start()
+    load_length = pltpu.make_async_copy(length_ref, lengthy, load_sem.at[2])
+    fetches = [
+        pltpu.make_async_copy(
+            storage_ref.at[:, columns(piece)], stored.at[:, columns(piece)], fetch_sem.at[piece]
+        )
+        for piece in range(pieces)
+    ]
+    load_table.start()
+    for fetch in fetches:
+        fetch.start()
     barrier = pltpu.get_barrier_semaphore()
     for step in range(1, batch_count):
         pl.semaphore_signal(
@@ -155,7 +169,11 @@
         )
     pl.semaphore_signal(barrier, inc=1, device_id={"heads": sibling}, device_id_type=MESH)
 
-    table = table_ref[...]
+    load_query.start()
+    load_length.start()
+
+    load_table.wait()
+    table = tabled[...]
     device_count = table.shape[0]
     row_ids = lax.broadcasted_iota(jnp.int32, table.shape, 0)
     square = (slot_count, slot_count)
@@ -169,58 +187,63 @@
     rank = jnp.sum(belongs * counts, axis=0, keepdims=True).astype(jnp.int32)
     place = owner * per_peer + rank
     order = (down == place).astype(jnp.float32).astype(jnp.bfloat16)
-    load_storage.wait()
-    piece = 4 * 128
-    for first in range(0, stored.shape[1], piece):
-        outgoing[:, first : first + piece] = jnp.dot(
-            order, stored[:, first : first + piece], preferred_element_type=jnp.float32
+
+    def group(piece):
+        fetches[piece].wait()
+        outgoing[:, columns(piece)] = jnp.dot(
+            order, stored[:, columns(piece)], preferred_element_type=jnp.float32
         ).astype(jnp.bfloat16)
-    pl.semaphore_wait(barrier, batch_count)
 
     def rows(index):
         return pl.ds(pl.multiple_of(index * per_peer, per_peer), per_peer)
 
-    def send(step):
+    def send(step, piece):
         other = partner(step)
         return pltpu.make_async_remote_copy(
-            src_ref=outgoing.at[rows(other)],
-            dst_ref=keys.at[0, rows(me)],
-            send_sem=send_sem.at[step],
-            recv_sem=recv_sem.at[step],
+            src_ref=outgoing.at[rows(other), columns(piece)],
+            dst_ref=keys.at[0, rows(me), columns(piece)],
+            send_sem=send_sem.at[piece, step],
+            recv_sem=recv_sem.at[piece, step],
             device_id={"batch": other},
             device_id_type=MESH,
         )
 
-    def arrival(step):
+    def arrival(step, piece):
         other = partner(step)
         return pltpu.make_async_remote_copy(
-            src_ref=outgoing.at[rows(other)],
-            dst_ref=keys.at[0, rows(other)],
-            send_sem=send_sem.at[step],
-            recv_sem=recv_sem.at[step],
+            src_ref=outgoing.at[rows(other), columns(piece)],
+            dst_ref=keys.at[0, rows(other), columns(piece)],
+            send_sem=send_sem.at[piece, step],
+            recv_sem=recv_sem.at[piece, step],
             device_id={"batch": other},
             device_id_type=MESH,
         )
 
-    def hand_over(step):
+    def hand_over(step, piece):
         other = partner(step)
-        source = outgoing.at[rows(me)] if step == 0 else keys.at[0, rows(other)]
+        source = outgoing if step == 0 else keys.at[0]
         return pltpu.make_async_remote_copy(
-            src_ref=source,
-            dst_ref=keys.at[1, rows(other)],
-            send_sem=pass_sem.at[step],
-            recv_sem=take_sem.at[step],
+            src_ref=source.at[rows(other), columns(piece)],
+            dst_ref=keys.at[1, rows(other), columns(piece)],
+            send_sem=pass_sem.at[piece, step],
+            recv_sem=take_sem.at[piece, step],
             device_id={"heads": sibling},
             device_id_type=MESH,
         )
 
-    steps = list(range(batch_count - 1, 0, -1))
-    for step in steps:
-        send(step).start()
-    hand_over(0).start()
-    keep = pltpu.make_async_copy(outgoing.at[rows(me)], keys.at[0, rows(me)], load_sem.at[2])
-    keep.start()
-
+    steps = list(range(1, batch_count))
+
+    def send_all(piece):
+        for step in steps:
+            send(step, piece).start()
+
+    group(0)
+    pl.semaphore_wait(barrier, batch_count)
+    send_all(0)
+    for piece in range(1, pieces):
+        group(piece)
+        if piece > 1:
+            send_all(piece - 1)
     mine = table // block_count == me
     marks = mine.astype(jnp.float32)
     ranks = jnp.dot(
@@ -242,10 +265,17 @@
         ],
         axis=1,
     ).astype(jnp.int32)
+    for piece in range(pieces):
+        hand_over(0, piece).start()
+    keep = pltpu.make_async_copy(outgoing.at[rows(me)], keys.at[0, rows(me)], load_sem.at[3])
+    keep.start()
+    send_all(pieces - 1)
+
     row_count = asked.shape[0]
     heads = row_count // QTOK
     draft = lax.broadcasted_iota(jnp.int32, (row_count, 1), 0) // heads
-    limits = length_ref[0] - QTOK + draft
+    load_length.wait()
+    limits = lengthy[0] - QTOK + draft
 
     load_query.wait()
     space = wide - width
@@ -254,46 +284,49 @@
     query_odd[:, space:] = asked[...]
     query_odd[:, :space] = jnp.zeros((row_count, space), jnp.bfloat16)
 
-    for step in steps:
-        arrival(step).wait_recv()
-        hand_over(step).start()
     keep.wait()
-    for step in [0] + steps:
-        hand_over(step).wait_recv()
-
     factor = math.log2(math.e) / math.sqrt(HEAD_NOPE + ROPE)
     both = 2 * slot_count
-    scores = []
-    for i in range(BLK):
-        low = i * width // 128 * 128
-        queries = query_odd if i % 2 else query_even
-        part = keys[:, :, low : low + wide].reshape(both, wide)
-        dots = lax.dot_general(queries[...], part, NT, preferred_element_type=jnp.float32)
-        visible = numbers * BLK + i <= limits
-        scores.append(jnp.where(visible, dots, -1e30))
-    peak = functools.reduce(jnp.maximum, scores)
-    peak = jnp.max(peak, axis=1, keepdims=True)
+    shifted = width // 128 * 128
+    peak = jnp.full((row_count, 1), -1e30, jnp.float32)
     totals = jnp.zeros((row_count, both), jnp.float32)
     mixed_even = jnp.zeros((row_count, LATENT), jnp.float32)
     mixed_odd = jnp.zeros((row_count, wide), jnp.float32)
-    for i in range(BLK):
-        low = i * width // 128 * 128
-        raised = jnp.exp2((scores[i] - peak) * factor)
-        totals += raised
-        weights = raised.astype(jnp.bfloat16)
-        if i % 2:
-            part = keys[:, :, low : low + wide].reshape(both, wide)
-            mixed_odd += jnp.dot(weights, part, preferred_element_type=jnp.float32)
-        else:
-            part = keys[:, :, low : low + LATENT].reshape(both, LATENT)
-            mixed_even += jnp.dot(weights, part, preferred_element_type=jnp.float32)
+    for piece in range(pieces):
+        for step in steps:
+            arrival(step, piece).wait_recv()
+            hand_over(step, piece).start()
+        for step in [0] + steps:
+            hand_over(step, piece).wait_recv()
+        base = piece * span
+        parts = [
+            keys[:, :, low : low + wide].reshape(both, wide) for low in (base, base + shifted)
+        ]
+        scores = []
+        for i, queries in enumerate((query_even, query_odd)):
+            dots = lax.dot_general(queries[...], parts[i], NT, preferred_element_type=jnp.float32)
+            visible = numbers * BLK + (2 * piece + i) <= limits
+            scores.append(jnp.where(visible, dots, -1e30))
+        higher = jnp.max(jnp.maximum(scores[0], scores[1]), axis=1, keepdims=True)
+        higher = jnp.maximum(peak, higher)
+        shrink = jnp.exp2((peak - higher) * factor)
+        peak = higher
+        raised = [jnp.exp2((one - peak) * factor) for one in scores]
+        totals = totals * shrink + (raised[0] + raised[1])
+        mixed_even = mixed_even * shrink + jnp.dot(
+            raised[0].astype(jnp.bfloat16), parts[0][:, :LATENT], preferred_element_type=jnp.float32
+        )
+        mixed_odd = mixed_odd * shrink + jnp.dot(
+            raised[1].astype(jnp.bfloat16), parts[1], preferred_element_type=jnp.float32
+        )
     total = jnp.sum(totals, axis=1, keepdims=True)
     mixed = mixed_even + mixed_odd[:, space : space + LATENT]
     out_ref[...] = (mixed / total).astype(out_ref.dtype)
-    for step in steps:
-        send(step).wait_send()
-    for step in [0] + steps:
-        hand_over(step).wait_send()
+    for piece in range(pieces):
+        for step in steps:
+            send(step, piece).wait_send()
+        for step in [0] + steps:
+            hand_over(step, piece).wait_send()
 
 
 def local(storage, block_table, lengths, query):
@@ -312,20 +345,23 @@
     context = pl.pallas_call(
         functools.partial(fused_kernel, batch_count),
         out_shape=jax.ShapeDtypeStruct((row_count, LATENT), jnp.bfloat16),
-        in_specs=[vmem, pl.BlockSpec(memory_space=pltpu.SMEM), anywhere, anywhere],
+        in_specs=[anywhere] * 4,
         out_specs=vmem,
         scratch_shapes=[
+            pltpu.VMEM((block_table.shape[0] // slot_count, slot_count), jnp.int32),
+            pltpu.SMEM(lengths.shape, jnp.int32),
             pltpu.VMEM((slot_count, BLK * width), jnp.bfloat16),
             pltpu.VMEM((row_count, width), jnp.bfloat16),
             pltpu.VMEM((slot_count, BLK * width), jnp.bfloat16),
             pltpu.VMEM((2, slot_count, BLK * width), jnp.bfloat16),
             pltpu.VMEM((row_count, wide), jnp.bfloat16),
             pltpu.VMEM((row_count, wide), jnp.bfloat16),
-            pltpu.SemaphoreType.DMA((3,)),
-            pltpu.SemaphoreType.DMA((batch_count,)),
-            pltpu.SemaphoreType.DMA((batch_count,)),
-            pltpu.SemaphoreType.DMA((batch_count,)),
-            pltpu.SemaphoreType.DMA((batch_count,)),
+            pltpu.SemaphoreType.DMA((4,)),
+            pltpu.SemaphoreType.DMA((BLK // 2,)),
+            pltpu.SemaphoreType.DMA((BLK // 2, batch_count)),
+            pltpu.SemaphoreType.DMA((BLK // 2, batch_count)),
+            pltpu.SemaphoreType.DMA((BLK // 2, batch_count)),
+            pltpu.SemaphoreType.DMA((BLK // 2, batch_count)),
         ],
         compiler_params=pltpu.CompilerParams(collective_id=0, has_side_effects=True),
     )(

time: 40.3 us -> 37.8 us (0.938)
  Pallas kernels: 37.8 us -> 35.3 us
    pallas_call x1, Pallas kernels: 37.8 us -> 35.3 us  [local(): pl.pallas_call(functools.partial(fused_kernel, batch_count), out_shape=ja...]
where the time goes in v2:
time: 37.8 us; the launch traced here: 37.6 us
  Pallas kernels  35.3 us (93%)
  local copies, waits for them, and re-layouts  1.67 us (4%)
  between operations  0.66 us (2%)
    pallas_call x1, Pallas kernels, local(): pl.pallas_call(functools.partial(fused_kernel, batch_count), out_shape=ja...  35.3 us
    unnamed x1, local copies, waits for them, and re-layouts  1.67 us

profile of v2, /device:TPU:1, one launch (start us, length us, event | category | flops | bytes accessed | tf_op | source)
XLA Modules:
  0.0 37.6 jit_solution(2719320891123873004)
XLA Ops:
  0.7 35.3 %shard_map.46 = bf16[256,512]{1,0:T(8,128)(2,1)} custom-call(s32[16,128]{1,0:T(8,128)} %bitcast.7, s32[1]{0:T(128)S(6)} %copy.6.length_ref, bf16[128,4608]{1,0:T(8,128)(2,1)} %bitcast.4, bf16[256,576]{1,0:T(8,128)(2,1)} %bitcast.6), custom_call_target="tpu_custom_call" | custom-call | tf_op jit(solution)/shard_map/pallas_call | solution.py:345
  36.0 1.7 %copy.7 = bf16[1,4,64,512]{3,2,1,0:T(8,128)(2,1)} copy(bf16[1,4,64,512]{3,2,1,0:T(8,128)(2,1)} %bitcast.5) | data formatting | bytes 524288

commit v3 on v2

--- a/solution.py
+++ b/solution.py
@@ -341,7 +341,7 @@
     row_count = QTOK * heads
     wide = -(-width // 128) * 128
     vmem = pl.BlockSpec(memory_space=pltpu.VMEM)
-    anywhere = pl.BlockSpec(memory_space=pl.ANY)
+    anywhere = pl.BlockSpec(memory_space=pltpu.HBM)
     context = pl.pallas_call(
         functools.partial(fused_kernel, batch_count),
         out_shape=jax.ShapeDtypeStruct((row_count, LATENT), jnp.bfloat16),
@@ -363,7 +363,7 @@
             pltpu.SemaphoreType.DMA((BLK // 2, batch_count)),
             pltpu.SemaphoreType.DMA((BLK // 2, batch_count)),
         ],
-        compiler_params=pltpu.CompilerParams(collective_id=0, has_side_effects=True),
+        compiler_params=pltpu.CompilerParams(collective_id=0, has_side_effects=True, vmem_limit_bytes=54800 * 1024),
     )(
         block_table.reshape(-1, slot_count),
         lengths,

time: 37.8 us -> 36.8 us (0.974)
  Pallas kernels: 35.3 us -> 34.5 us
    pallas_call x1, Pallas kernels: 35.3 us -> 34.5 us  [local(): pl.pallas_call(functools.partial(fused_kernel, batch_count), out_shape=ja...]
    unnamed x1 -> x3, local copies, waits for them, and re-layouts: 1.67 us -> 1.4 us
where the time goes in v3:
time: 36.8 us; the launch traced here: 36.6 us
  Pallas kernels  34.5 us (94%)
  local copies, waits for them, and re-layouts  1.4 us (4%)
  between operations  0.67 us (2%)
    pallas_call x1, Pallas kernels, local(): pl.pallas_call(functools.partial(fused_kernel, batch_count), out_shape=ja...  34.5 us
    unnamed x3, local copies, waits for them, and re-layouts  1.4 us

profile of v3, /device:TPU:1, one launch (start us, length us, event | category | flops | bytes accessed | tf_op | source)
XLA Modules:
  0.0 36.6 jit_solution(11268339542790255241)
XLA Ops:
  0.7 0.0 copy-start
  0.7 0.7 %copy-done = s32[2048]{0:T(1024)S(1)} copy-done((s32[2048]{0:T(1024)S(1)}, s32[2048]{0:T(1024)}, u32[]{:S(2)}) %copy-start) | copy-done | bytes 8216
  1.4 34.5 %shard_map.46 = bf16[256,512]{1,0:T(8,128)(2,1)S(1)} custom-call(s32[16,128]{1,0:T(8,128)S(1)} %bitcast.5, s32[1]{0:T(128)S(6)} %copy.6.length_ref, bf16[128,4608]{1,0:T(8,128)(2,1)} %bitcast.6, bf16[256,576]{1,0:T(8,128)(2,1)} %bitcast.7), custom_call_target="tpu_custom_call" | custom-call | tf_op jit(solution)/shard_map/pallas_call | solution.py:345
  35.9 0.7 %copy.7 = bf16[1,4,64,512]{3,2,1,0:T(8,128)(2,1)} copy(bf16[1,4,64,512]{3,2,1,0:T(8,128)(2,1)S(1)} %bitcast.4) | data formatting | bytes 524288
Async XLA Ops:
  0.7 0.7 %copy-start = (s32[2048]{0:T(1024)S(1)}, s32[2048]{0:T(1024)}, u32[]{:S(2)}) copy-start(s32[2048]{0:T(1024)} %param.5) | copy-start | bytes 24580
